TPU v7x, 256 devices: a whole 4x4x8 slice. The times are simulated.
256 devices in a mesh: dp: 64 (over y, z_hi, x), tensor: 4 (over z_lo, core).
Axes of the slice: x: 4, y: 4, z: 8 (z_hi: 4, z_lo: 2; z = z_hi * 2 + z_lo), core: 2. Of those that a mesh axis runs over, the one named last changes fastest.
Arguments:
- activations: bfloat16 [32768, 4096], P('dp'), may hold values from -1000 to 1000
- norm_gain: bfloat16 [4096], replicated, may hold values from 0.5 to 1.5
- query_blocks: bfloat16 [128, 32, 4096], P('dp', None, 'tensor'), may hold values from -64 to 64
- query_scales: int32 [128, 1, 4096], P('dp', None, 'tensor'), may hold values from -9 to -5
- key_blocks: bfloat16 [128, 32, 512], P('dp', None, 'tensor'), may hold values from -64 to 64
- key_scales: int32 [128, 1, 512], P('dp', None, 'tensor'), may hold values from -9 to -5
- value_blocks: bfloat16 [128, 32, 512], P('dp', None, 'tensor'), may hold values from -6 to 6
- value_scales: int32 [128, 1, 512], P('dp', None, 'tensor'), may hold values from -9 to -5
- output_blocks: bfloat16 [128, 32, 4096], P('tensor', None, 'dp'), may hold values from -6 to 6
- output_scales: int32 [128, 1, 4096], P('tensor', None, 'dp'), may hold values from -9 to -5
Outputs:
- attended: bfloat16 [32768, 4096], P('dp')
All inputs are finite; a program needn't handle non-finite values.
Results may differ from a plain program's by a relative error of at most 0.015.
The roundings to bfloat16 on the way count: a program that leaves them out, or rounds other values in their place, can miss the bound.
Values may be sent and summed in bfloat16 or wider, within the bound.
A program may use at most 128 MiB of HBM per device.

v0:
```python
import math
import jax
import jax.numpy as jnp
from jax import lax
from jax.sharding import PartitionSpec as P

HEAD_DIM = 128
SEQ = 256
EPS = 1e-05
ROPE_BASE = 500000.0


def turned_gather(arrays, axis, dims):
    turned = [jnp.moveaxis(a, dim, 0) for a, dim in zip(arrays, dims)]
    widths = [t[0].size for t in turned]
    both = jnp.concatenate([t.reshape(-1, w) for t, w in zip(turned, widths)], axis=1)
    out = lax.all_gather(both, axis, axis=0, tiled=True)
    blocks = jnp.split(out, [sum(widths[:k]) for k in range(1, len(widths))], axis=1)
    return tuple(
        (
            jnp.moveaxis(b.reshape(-1, *t.shape[1:]), 0, dim)
            for b, t, dim in zip(blocks, turned, dims)
        )
    )


def side_by_side(arrays, axis, dim, along):
    widths = [math.prod(a.shape[along:]) for a in arrays]
    both = jnp.concatenate(
        [a.reshape(*a.shape[:along], w) for a, w in zip(arrays, widths)], axis=along
    )
    out = lax.all_gather(both, axis, axis=dim, tiled=True)
    blocks = jnp.split(out, [sum(widths[:k]) for k in range(1, len(widths))], axis=along)
    return tuple((b.reshape(*out.shape[:along], *a.shape[along:]) for a, b in zip(arrays, blocks)))


def dequant(blocks, scales):
    factor = jnp.exp2(scales.astype(jnp.float32)).astype(blocks.dtype)
    weight = blocks * factor
    return weight.reshape(weight.shape[0] * weight.shape[1], weight.shape[2])


def rotate_pairs(states, positions):
    half_dim = states.shape[-1] // 2
    frequency = jnp.exp(
        -math.log(ROPE_BASE) * jnp.arange(half_dim, dtype=jnp.float32) * 2.0 / states.shape[-1]
    )
    angles = positions.astype(jnp.float32)[:, None] * frequency[None, :]
    cosine = jnp.cos(angles)[None, :, None, :]
    sine_part = jnp.sin(angles)[None, :, None, :]
    first = states[..., :half_dim]
    second = states[..., half_dim:]
    return jnp.concatenate(
        [first * cosine - second * sine_part, second * cosine + first * sine_part], axis=-1
    )


def attend(query_states, key_states, value_states, kv_count):
    tokens_here = query_states.shape[0]
    count = tokens_here // SEQ
    positions = jnp.arange(SEQ, dtype=jnp.int32)
    queries = rotate_pairs(query_states.reshape(count, SEQ, -1, HEAD_DIM), positions).astype(
        jnp.bfloat16
    )
    rotated_keys = rotate_pairs(
        key_states.reshape(count, SEQ, kv_count, HEAD_DIM), positions
    ).astype(jnp.bfloat16)
    value_heads = value_states.astype(jnp.bfloat16).reshape(count, SEQ, kv_count, HEAD_DIM)
    group_size = queries.shape[2] // kv_count
    queries = queries.reshape(count, SEQ, kv_count, group_size, HEAD_DIM)
    scores = jnp.einsum(
        "sqkgd,stkd->skgqt", queries, rotated_keys, preferred_element_type=jnp.float32
    ) * HEAD_DIM ** (-0.5)
    visible = positions[:, None] >= positions[None, :]
    scores = jnp.where(visible, scores, -jnp.inf)
    attn_weights = jax.nn.softmax(scores, axis=-1).astype(jnp.bfloat16)
    context = jnp.einsum(
        "skgqt,stkd->sqkgd", attn_weights, value_heads, preferred_element_type=jnp.float32
    )
    return context.astype(jnp.bfloat16).reshape(tokens_here, -1)


def shards(
    activations,
    norm_gain,
    query_blocks,
    query_scales,
    key_blocks,
    key_scales,
    value_blocks,
    value_scales,
    output_blocks,
    output_scales,
):
    query_exps = query_scales.astype(jnp.bfloat16)
    key_exps = key_scales.astype(jnp.bfloat16)
    value_exps = value_scales.astype(jnp.bfloat16)
    output_exps = output_scales.astype(jnp.bfloat16)
    output_whole = turned_gather((output_blocks, output_exps), "dp", (2, 2))
    wide_rows = activations.astype(jnp.float32)
    inverse = lax.rsqrt(jnp.mean(wide_rows * wide_rows, axis=-1, keepdims=True) + EPS)
    normed = (wide_rows * inverse * norm_gain.astype(jnp.float32)).astype(jnp.bfloat16)

    def product(blocks, scales):
        return jnp.dot(normed, dequant(blocks, scales), preferred_element_type=jnp.float32)

    pieces = side_by_side(
        (query_blocks, query_exps, key_blocks, key_exps, value_blocks, value_exps), "dp", 0, 1
    )
    query_states = product(pieces[0], pieces[1])
    key_states = product(pieces[2], pieces[3])
    value_states = product(pieces[4], pieces[5])
    context = attend(query_states, key_states, value_states, key_blocks.shape[2] // HEAD_DIM)
    partial_value = jnp.dot(
        context, dequant(output_whole[0], output_whole[1]), preferred_element_type=jnp.float32
    )
    return lax.psum(partial_value.astype(jnp.bfloat16), "tensor")


def solution(mesh):
    placed = (
        P("dp", None),
        P(),
        P("dp", None, "tensor"),
        P("dp", None, "tensor"),
        P("dp", None, "tensor"),
        P("dp", None, "tensor"),
        P("dp", None, "tensor"),
        P("dp", None, "tensor"),
        P("tensor", None, "dp"),
        P("tensor", None, "dp"),
    )
    return jax.shard_map(
        shards, mesh=mesh, in_specs=placed, out_specs=P("dp", None), check_vma=False
    )
```

profile of v0, /device:TPU:1, one launch (start us, length us, event | category | flops | bytes accessed | tf_op | source)
XLA Modules:
  0.0 459.1 jit_solution(9904622550752400796)
XLA Ops:
  6.5 0.0 all-gather.4.cloned.1.call-start
  6.5 0.7 convert_bitcast_fusion
  7.3 1.0 pad_maximum_fusion
  8.3 0.8 copy.48
  9.1 0.0 all-gather.4.cloned.1.call-update
  9.1 0.0 all-gather.6.cloned.1.call-start
  9.2 1.0 copy.64
  10.2 0.1 constant_dynamic-update-slice_fusion.3
  10.3 0.7 constant_dynamic-update-slice_fusion.2
  11.0 0.7 bitcast_dynamic-update-slice_fusion.1
  11.8 0.7 constant_dynamic-update-slice_fusion.1
  12.4 0.7 bitcast_dynamic-update-slice_fusion
  13.2 0.7 constant_dynamic-update-slice_fusion
  13.9 0.0 copy-start.2
  13.9 0.7 copy-done.2
  14.6 0.0 all-gather.6.cloned.1.call-update
  14.6 0.0 all-reduce.2.cloned.1.call-start
  14.6 0.0 copy-start
  14.6 0.9 convert_element_type.104
  15.5 3.3 fusion
  18.9 0.3 multiply_cosine_fusion
  19.2 0.0 copy-done
  19.2 3.6 fusion.2
  22.8 106.9 %all-gather.4.cloned.1.call-done = bf16[4096,1056]{1,0:T(8,128)(2,1)} async-done(((bf16[64,1056]{1,0:T(8,128)(2,1)}), bf16[4096,1056]{1,0:T(8,128)(2,1)}) %all-gather.4.cloned.1.call-update) | async-done | bytes 8650768 | tf_op jit(solution)/shard_map/all_gather | solution.py:17
  129.7 1.6 fusion.14
  131.3 0.3 copy.50
  131.6 7.7 %split.38 = bf16[4096,1024]{1,0:T(8,128)(2,1)} slice(bf16[4096,1056]{1,0:T(8,128)(2,1)} %all-gather.4.cloned.1.call-done), slice={[0:4096], [0:1024]} | slice | bytes 16777216 | tf_op jit(solution)/shard_map/split | solution.py:18
  139.3 11.4 %copy.63 = bf16[4096,1024]{0,1:T(8,128)(2,1)} copy(bf16[4096,1024]{1,0:T(8,128)(2,1)} %split.38) | data formatting | bytes 16777216
  150.7 7.4 %broadcast_multiply_fusion = bf16[32,32,4096]{2,1,0:T(8,128)(2,1)} fusion(bf16[32,32,4096]{2,1,0:T(8,128)(2,1)} %bitcast.115, bf16[32,4096]{1,0:T(8,128)(2,1)S(1)} %copy.50), kind=kLoop, calls=%fused_computation.8 | loop fusion | flops 4194304 | bytes 17039360 | tf_op jit(solution)/shard_map/mul | solution.py:39
  158.1 97.6 %all-gather.6.cloned.1.call-done = bf16[64,2,42240]{2,1,0:T(2,128)(2,1)} async-done(((bf16[1,2,42240]{2,1,0:T(2,128)(2,1)}), bf16[64,2,42240]{2,1,0:T(2,128)(2,1)}) %all-gather.6.cloned.1.call-update) | async-done | bytes 10813456 | tf_op jit(solution)/shard_map/all_gather | solution.py:32
  255.7 14.6 %reshape.197 = bf16[128,42240]{1,0:T(8,128)(2,1)} reshape(bf16[64,2,42240]{2,1,0:T(2,128)(2,1)} %all-gather.6.cloned.1.call-done) | data formatting | bytes 21626880
  270.4 0.8 exponential_convert_fusion.2
  271.2 1.0 exponential_convert_fusion.1
  272.2 7.3 %split.36 = bf16[128,32768]{1,0:T(8,128)(2,1)} slice(bf16[128,42240]{1,0:T(8,128)(2,1)} %reshape.197), slice={[0:128], [0:32768]} | slice | bytes 16777216 | tf_op jit(solution)/shard_map/split | solution.py:33
  279.5 0.1 mul.220
  279.7 1.9 bitcast_multiply_fusion.1
  281.6 13.5 %reshape.189 = bf16[4096,1024]{1,0:T(8,128)(2,1)} reshape(bf16[128,32768]{1,0:T(8,128)(2,1)} %split.36) | data formatting | bytes 16777216 | tf_op jit(solution)/shard_map/reshape | solution.py:34
  295.1 7.2 %bitcast_multiply_fusion = bf16[4096,1024]{1,0:T(8,128)(2,1)} fusion(bf16[4096,1024]{1,0:T(8,128)(2,1)} %reshape.189, bf16[128,1024]{1,0:T(8,128)(2,1)S(1)} %exponential_convert_fusion.1), kind=kLoop, calls=%fused_computation.5 | loop fusion | flops 4194304 | bytes 17039360 | tf_op jit(solution)/shard_map/mul | solution.py:39
  302.3 11.4 %copy.62 = bf16[1024,4096]{1,0:T(8,128)(2,1)} copy(bf16[1024,4096]{0,1:T(8,128)(2,1)} %bitcast.116) | data formatting | bytes 16777216 | tf_op jit(solution)/shard_map/dot_general | solution.py:105
  313.7 0.5 mul.223
  314.3 0.5 reshape.187
  314.8 0.0 copy-start.1
  314.8 0.1 bitcast_multiply_fusion.2
  314.9 3.6 convolution_convert_fusion.1
  318.5 0.0 copy-done.1
  318.5 7.4 %fusion.30 = f32[2,256,8,128]{1,3,2,0:T(8,128)S(1)} fusion(bf16[2,256,4096,1]{2,1,3,0:T(8,128)(2,1)S(1)} %bitcast.117, bf16[8,128,4096,1]{2,1,0,3:T(8,128)(2,1)} %bitcast.120), kind=kOutput, calls=%fused_computation.62 | convolution fusion | flops 4294967296 | bytes 14680064 | tf_op jit(solution)/shard_map/dot_general | solution.py:105
  325.9 1.5 convolution_bitcast_fusion
  327.4 0.3 subtract_convert_fusion
  327.8 0.8 fusion.4
  328.6 0.9 fusion.3
  329.5 1.3 fusion.11
  330.8 0.8 copy.46
  331.6 9.4 %convolution_convert_fusion = bf16[512,4096]{1,0:T(8,128)(2,1)} fusion(bf16[1024,4096]{1,0:T(8,128)(2,1)} %bitcast.119, bf16[64,8,8,128]{3,2,1,0:T(8,128)(2,1)S(1)} %bitcast.122), kind=kOutput, calls=%fused_computation.6 | convolution fusion | flops 4297064448 | bytes 13631488 | tf_op jit(solution)/shard_map/dot_general | solution.py:114
  341.0 0.0 all-reduce.2.cloned.1.call-update
  341.0 106.9 %all-reduce.2.cloned.1.call-done = bf16[512,4096]{1,0:T(8,128)(2,1)} async-done(((bf16[512,4096]{1,0:T(8,128)(2,1)}), bf16[512,4096]{1,0:T(8,128)(2,1)}) %all-reduce.2.cloned.1.call-update) | async-done | bytes 4194320 | tf_op jit(solution)/shard_map/psum | solution.py:117
  447.9 4.7 %copy.87 = bf16[512,4096]{1,0:T(8,128)(2,1)} copy(bf16[512,4096]{1,0:T(8,128)(2,1)} %all-reduce.2.cloned.1.call-done) | data formatting | bytes 8388608
  (5 shorter events, 0.1 us)
Async XLA Ops:
  6.5 123.2 %all-gather.4.cloned.1.call-start = ((), (), s32[]{:S(2)}) async-start(), calls=%async_computation | async-start | bytes 9584640 | tf_op jit(solution)/shard_map/all_gather | solution.py:17
  9.1 246.6 %all-gather.6.cloned.1.call-start = ((), (), s32[]{:S(2)}) async-start(), calls=%async_computation.2 | async-start | bytes 10982400 | tf_op jit(solution)/shard_map/all_gather | solution.py:32
  13.9 0.7 copy-start.2
  14.6 433.3 %all-reduce.2.cloned.1.call-start = ((), (), s32[]{:S(2)}) async-start(), calls=%async_computation.1 | async-start | bytes 8388608 | tf_op jit(solution)/shard_map/psum | solution.py:117
  14.6 4.5 copy-start
  314.8 3.7 copy-start.1
Sparse Core Ops, SparseCore 0:
  10.5 119.1 all-gather.3
  133.0 122.6 all-gather.5
  341.1 106.7 all-reduce.1
where the time goes:
time: 461 us; the launch traced here: 459 us
  waiting for transfers between devices  311 us (67%)
  local copies, waits for them, and re-layouts  77 us (17%)
  other arithmetic  33.3 us (7%)
  matrix products  24 us (5%)
  between operations  13.3 us (3%)
    all_gather x1, waiting for transfers between devices, turned_gather(): out = lax.all_gather(both, axis, axis=0, tiled=True)  107 us
    psum x1, waiting for transfers between devices, shards(): return lax.psum(partial_value.astype(jnp.bfloat16), 'tensor')  107 us
    all_gather x1, waiting for transfers between devices, side_by_side(): out = lax.all_gather(both, axis, axis=dim, tiled=True)  97.6 us
    unnamed x13, local copies, waits for them, and re-layouts  34 us
    mul x5, other arithmetic, dequant(): weight = blocks * factor  18.2 us
    reshape x2, local copies, waits for them, and re-layouts, side_by_side(): b.reshape(*out.shape[:along], *a.shape[along:])  14 us
    dot_general x3, matrix products, product(): jnp.dot(normed, dequant(blocks, scales), preferred_element_type=jnp.float32)  12.5 us
    dot_general x1, local copies, waits for them, and re-layouts, product(): jnp.dot(normed, dequant(blocks, scales), preferred_element_type=jnp.float32)  11.4 us
  transfers between devices with their start and end apart: 3, of which 3 were waited for; matrix products, arithmetic and copies ran while one was open for 9% of the time, Pallas kernels for 0%

commit v1 on v0

--- a/solution.py
+++ b/solution.py
@@ -14,7 +14,10 @@
     turned = [jnp.moveaxis(a, dim, 0) for a, dim in zip(arrays, dims)]
     widths = [t[0].size for t in turned]
     both = jnp.concatenate([t.reshape(-1, w) for t, w in zip(turned, widths)], axis=1)
-    out = lax.all_gather(both, axis, axis=0, tiled=True)
+    size = lax.axis_size(axis)
+    parts = jnp.stack([both for _ in range(size)])
+    parts = lax.all_to_all(parts, axis, split_axis=0, concat_axis=0)
+    out = jnp.concatenate(parts, axis=0)
     blocks = jnp.split(out, [sum(widths[:k]) for k in range(1, len(widths))], axis=1)
     return tuple(
         (

time: 461 us -> 542 us (1.18)
  waiting for transfers between devices: 311 us -> 373 us
  starting transfers between devices: 0.09 us -> 15.5 us
    all_to_all x0 -> x1, waiting for transfers between devices: none -> 265 us  [turned_gather(): parts = lax.all_to_all(parts, axis, split_axis=0, concat_axis=0)]
    all_gather x1 -> x0, waiting for transfers between devices: 107 us -> none  [turned_gather(): out = lax.all_gather(both, axis, axis=0, tiled=True)]
    all_gather x1, waiting for transfers between devices: 97.6 us -> 0.01 us  [side_by_side(): out = lax.all_gather(both, axis, axis=dim, tiled=True)]
    all_to_all x0 -> x1, starting transfers between devices: none -> 15.5 us  [turned_gather(): parts = lax.all_to_all(parts, axis, split_axis=0, concat_axis=0)]
    split x1 -> x2, local copies, waits for them, and re-layouts: 7.67 us -> 19.2 us  [turned_gather(): jnp.split(out, [sum(widths[:k]) for k in range(1, len(widths))], axis=1)]
    unnamed x13 -> x14, local copies, waits for them, and re-layouts: 34 us -> 22.7 us
  transfers between devices with their start and end apart: 3 -> 3, of which waited for: 3 -> 2; matrix products, arithmetic and copies ran while one was open for 9% -> 8% of each run, Pallas kernels for 0% -> 0%
where the time goes in v1:
time: 542 us; the launch traced here: 540 us
  waiting for transfers between devices  373 us (69%)
  local copies, waits for them, and re-layouts  81.5 us (15%)
  other arithmetic  32.3 us (6%)
  matrix products  24 us (4%)
  starting transfers between devices  15.5 us (3%)
  between operations  13.6 us (3%)
    all_to_all x1, waiting for transfers between devices, turned_gather(): parts = lax.all_to_all(parts, axis, split_axis=0, concat_axis=0)  265 us
    psum x1, waiting for transfers between devices, shards(): return lax.psum(partial_value.astype(jnp.bfloat16), 'tensor')  108 us
    unnamed x14, local copies, waits for them, and re-layouts  22.7 us
    split x2, local copies, waits for them, and re-layouts, turned_gather(): jnp.split(out, [sum(widths[:k]) for k in range(1, len(widths))], axis=1)  19.2 us
    mul x5, other arithmetic, dequant(): weight = blocks * factor  18.1 us
    all_to_all x1, starting transfers between devices, turned_gather(): parts = lax.all_to_all(parts, axis, split_axis=0, concat_axis=0)  15.5 us
    reshape x2, local copies, waits for them, and re-layouts, side_by_side(): b.reshape(*out.shape[:along], *a.shape[along:])  14 us
    dot_general x3, matrix products, product(): jnp.dot(normed, dequant(blocks, scales), preferred_element_type=jnp.float32)  12.5 us
  transfers between devices with their start and end apart: 3, of which 2 were waited for; matrix products, arithmetic and copies ran while one was open for 8% of the time, Pallas kernels for 0%

profile of v1, /device:TPU:1, one launch (start us, length us, event | category | flops | bytes accessed | tf_op | source)
XLA Modules:
  0.0 540.1 jit_solution(4302217105830840284)
XLA Ops:
  6.5 0.0 all-gather.3.cloned.1.call-start
  6.5 1.0 copy.62
  7.6 0.1 constant_dynamic-update-slice_fusion.3
  7.7 0.7 constant_dynamic-update-slice_fusion.2
  8.4 0.7 bitcast_dynamic-update-slice_fusion.1
  9.1 0.7 constant_dynamic-update-slice_fusion.1
  9.8 0.7 bitcast_dynamic-update-slice_fusion
  10.6 0.7 constant_dynamic-update-slice_fusion
  11.2 0.0 copy-start.2
  11.2 0.7 copy-done.2
  11.9 0.0 all-gather.3.cloned.1.call-update
  12.0 0.7 convert_bitcast_fusion
  12.7 1.0 pad_maximum_fusion
  13.7 0.2 copy.47
  13.9 4.9 stack.2
  18.8 0.0 copy-start.3
  18.8 15.5 %all-to-all-start = ((bf16[64,64,1056]{2,1,0:T(8,128)(2,1)}), bf16[64,64,1056]{2,1,0:T(8,128)(2,1)}, u32[]{:S(2)}, u32[]{:S(2)}) async-start(bf16[64,64,1056]{2,1,0:T(8,128)(2,1)} %stack.2), calls=%async_computation | async-start | bytes 18874368 | tf_op jit(solution)/shard_map/all_to_all | solution.py:19
  34.2 0.0 all-reduce.2.cloned.1.call-start
  34.3 0.0 copy-done.3
  34.3 0.0 copy-start
  34.4 3.3 fusion
  37.7 0.3 multiply_cosine_fusion
  38.0 0.0 copy-done
  38.0 3.6 fusion.2
  41.6 265.4 %all-to-all-done = bf16[64,64,1056]{2,1,0:T(8,128)(2,1)} async-done(((bf16[64,64,1056]{2,1,0:T(8,128)(2,1)}), bf16[64,64,1056]{2,1,0:T(8,128)(2,1)}, u32[]{:S(2)}, u32[]{:S(2)}) %all-to-all-start) | async-done | bytes 8650784 | tf_op jit(solution)/shard_map/all_to_all | solution.py:19
  307.1 7.7 %split.38 = bf16[4096,1024]{1,0:T(8,128)(2,1)} slice(bf16[4096,1056]{1,0:T(8,128)(2,1)} %bitcast.31), slice={[0:4096], [0:1024]} | slice | bytes 16777216 | tf_op jit(solution)/shard_map/split | solution.py:21
  314.8 1.6 fusion.14
  316.3 0.3 copy.49
  316.6 11.6 %copy.48 = bf16[4096,1024]{0,1:T(8,128)(2,1)} copy(bf16[4096,1024]{1,0:T(8,128)(2,1)} %split.38) | data formatting | bytes 16777216 | tf_op jit(solution)/shard_map/split | solution.py:21
  328.2 7.3 %broadcast_multiply_fusion = bf16[32,32,4096]{2,1,0:T(8,128)(2,1)} fusion(bf16[32,32,4096]{2,1,0:T(8,128)(2,1)} %bitcast.116, bf16[32,4096]{1,0:T(8,128)(2,1)S(1)} %copy.49), kind=kLoop, calls=%fused_computation.8 | loop fusion | flops 4194304 | bytes 17039360 | tf_op jit(solution)/shard_map/mul | solution.py:42
  335.6 0.0 all-gather.3.cloned.1.call-done
  335.6 14.6 %reshape.203 = bf16[128,42240]{1,0:T(8,128)(2,1)} reshape(bf16[64,2,42240]{2,1,0:T(2,128)(2,1)} %all-gather.3.cloned.1.call-done) | data formatting | bytes 21626880
  350.2 0.8 exponential_convert_fusion.2
  351.0 1.0 exponential_convert_fusion.1
  352.1 7.3 %split.36 = bf16[128,32768]{1,0:T(8,128)(2,1)} slice(bf16[128,42240]{1,0:T(8,128)(2,1)} %reshape.203), slice={[0:128], [0:32768]} | slice | bytes 16777216 | tf_op jit(solution)/shard_map/split | solution.py:36
  359.4 0.1 mul.220
  359.5 1.9 bitcast_multiply_fusion.1
  361.5 13.5 %reshape.194 = bf16[4096,1024]{1,0:T(8,128)(2,1)} reshape(bf16[128,32768]{1,0:T(8,128)(2,1)} %split.36) | data formatting | bytes 16777216 | tf_op jit(solution)/shard_map/reshape | solution.py:37
  375.0 7.2 %bitcast_multiply_fusion = bf16[4096,1024]{1,0:T(8,128)(2,1)} fusion(bf16[4096,1024]{1,0:T(8,128)(2,1)} %reshape.194, bf16[128,1024]{1,0:T(8,128)(2,1)S(1)} %exponential_convert_fusion.1), kind=kLoop, calls=%fused_computation.5 | loop fusion | flops 4194304 | bytes 17039360 | tf_op jit(solution)/shard_map/mul | solution.py:42
  382.2 11.4 %copy.61 = bf16[1024,4096]{1,0:T(8,128)(2,1)} copy(bf16[1024,4096]{0,1:T(8,128)(2,1)} %bitcast.117) | data formatting | bytes 16777216 | tf_op jit(solution)/shard_map/dot_general | solution.py:108
  393.6 0.5 mul.223
  394.1 0.5 reshape.192
  394.7 0.0 copy-start.1
  394.7 0.1 bitcast_multiply_fusion.2
  394.8 3.6 convolution_convert_fusion.1
  398.4 0.0 copy-done.1
  398.4 7.4 %fusion.30 = f32[2,256,8,128]{1,3,2,0:T(8,128)S(1)} fusion(bf16[2,256,4096,1]{2,1,3,0:T(8,128)(2,1)S(1)} %bitcast.118, bf16[8,128,4096,1]{2,1,0,3:T(8,128)(2,1)} %bitcast.121), kind=kOutput, calls=%fused_computation.62 | convolution fusion | flops 4294967296 | bytes 14680064 | tf_op jit(solution)/shard_map/dot_general | solution.py:108
  405.7 1.5 convolution_bitcast_fusion
  407.3 0.3 subtract_convert_fusion
  407.7 0.8 fusion.4
  408.5 0.9 fusion.3
  409.4 1.3 fusion.11
  410.7 0.8 copy.45
  411.4 9.4 %convolution_convert_fusion = bf16[512,4096]{1,0:T(8,128)(2,1)} fusion(bf16[1024,4096]{1,0:T(8,128)(2,1)} %bitcast.120, bf16[64,8,8,128]{3,2,1,0:T(8,128)(2,1)S(1)} %bitcast.123), kind=kOutput, calls=%fused_computation.6 | convolution fusion | flops 4297064448 | bytes 13631488 | tf_op jit(solution)/shard_map/dot_general | solution.py:117
  420.8 0.0 all-reduce.2.cloned.1.call-update
  420.9 107.7 %all-reduce.2.cloned.1.call-done = bf16[512,4096]{1,0:T(8,128)(2,1)} async-done(((bf16[512,4096]{1,0:T(8,128)(2,1)}), bf16[512,4096]{1,0:T(8,128)(2,1)}) %all-reduce.2.cloned.1.call-update) | async-done | bytes 4194320 | tf_op jit(solution)/shard_map/psum | solution.py:120
  528.5 4.7 copy.85
  (6 shorter events, 0.1 us)
Async XLA Ops:
  6.5 329.0 %all-gather.3.cloned.1.call-start = ((), (), s32[]{:S(2)}) async-start(), calls=%async_computation.2 | async-start | bytes 10982400 | tf_op jit(solution)/shard_map/all_gather | solution.py:35
  11.2 0.7 copy-start.2
  18.8 15.5 %copy-start.3 = (bf16[4096]{0:T(1024)(128)(2,1)S(1)}, bf16[4096]{0:T(1024)(128)(2,1)}, u32[]{:S(2)}) copy-start(bf16[4096]{0:T(1024)(128)(2,1)} %param.11) | copy-start | bytes 24580
  18.8 288.3 %all-to-all-start = ((bf16[64,64,1056]{2,1,0:T(8,128)(2,1)}), bf16[64,64,1056]{2,1,0:T(8,128)(2,1)}, u32[]{:S(2)}, u32[]{:S(2)}) async-start(bf16[64,64,1056]{2,1,0:T(8,128)(2,1)} %stack.2), calls=%async_computation | async-start | bytes 18874368 | tf_op jit(solution)/shard_map/all_to_all | solution.py:19
  34.2 494.3 %all-reduce.2.cloned.1.call-start = ((), (), s32[]{:S(2)}) async-start(), calls=%async_computation.1 | async-start | bytes 8388608 | tf_op jit(solution)/shard_map/psum | solution.py:120
  34.3 3.7 copy-start
  394.7 3.7 copy-start.1
Sparse Core Ops, SparseCore 0:
  12.1 298.6 all-gather.2
  421.0 107.4 all-reduce.1
